TPU v7x, 128 devices: a whole 4x4x4 slice. The times are simulated.
128 devices in a mesh: band: 8 (over y, x_lo), chan: 16 (over x_hi, z, core).
Axes of the slice: x: 4 (x_hi: 2, x_lo: 2; x = x_hi * 2 + x_lo), y: 4, z: 4, core: 2. Of those that a mesh axis runs over, the one named last changes fastest.
Arguments:
- coeffs: bfloat16 [2, 8, 1024, 8192], P(None, None, 'chan', 'band'), may hold values from -1100 to 1100, as said below
Outputs:
- coherence: float32 [1024, 1024], P('chan', 'band')
Inputs may be any that keep to these rules, and one draw needn't show every extreme that they name: `coeffs`: finite real and imaginary parts.
All inputs are finite; a program needn't handle non-finite values.
Results may differ from a plain program's by a relative error of at most 0.0003.
Values may be sent and summed in bfloat16 or wider, within the bound.
A program may use at most 192 MiB of HBM per device.

v0:
```python
import jax
import jax.numpy as jnp
from jax import lax
from jax.sharding import PartitionSpec as P

K = 8
W = 16
epsilon = 1e-06


def in_blocks(shard, dim, length):
    dims = shard.shape
    tiles = shard.reshape(*dims[:dim], length, dims[dim] // length, *dims[dim + 1 :])
    return jnp.moveaxis(tiles, dim, 0)


def sent_and_summed(shard, axis, dim):
    length = lax.axis_size(axis)
    tiles = lax.all_to_all(in_blocks(shard, dim, length), axis, 0, 0, tiled=True)
    return jnp.sum(tiles, axis=0)


def body(coeffs):
    num_bands = coeffs.shape[3] // W
    own_width = coeffs.shape[2]
    cycle_size = lax.axis_size("chan")
    own_index = lax.axis_index("chan")
    full_width = own_width * cycle_size
    group_count = lax.axis_size("band")
    scale = jnp.float32(W * K / (num_bands * group_count))
    local_rows = coeffs.reshape(2, K, own_width, num_bands, W)
    paired = jnp.stack((local_rows[1], -local_rows[0]), axis=0)
    left_side = jnp.concatenate((local_rows, paired), axis=2)
    wide_rows = local_rows.astype(jnp.float32)
    own_power = jnp.sum(wide_rows * wide_rows, axis=(0, 1, 4)).T + epsilon
    piece = lax.all_gather(coeffs, "chan", axis=2, tiled=True)
    count = piece.shape[2]
    right_side = piece.reshape(2, K, count, num_bands, W)
    product = jnp.einsum(
        "pkinw,pkjnw->nij", left_side, right_side, preferred_element_type=jnp.float32
    )
    real_part = product[:, :own_width, :]
    imag_part = product[:, own_width:, :]
    wide_piece = right_side.astype(jnp.float32)
    piece_power = jnp.sum(wide_piece * wide_piece, axis=(0, 1, 4)).T + epsilon
    coh_band = (real_part * real_part + imag_part * imag_part) / (
        own_power[:, :, None] * piece_power[:, None, :]
    )
    partial_value = jnp.sum(coh_band, axis=0)
    row_global = lax.broadcasted_iota(jnp.int32, (own_width, full_width), 0) + own_index * own_width
    col_global = lax.broadcasted_iota(jnp.int32, (own_width, full_width), 1)
    partial_value = jnp.where(row_global == col_global, jnp.float32(0.0), partial_value)
    result = sent_and_summed(partial_value, "band", 1)
    return result * scale


def solution(mesh):
    return jax.shard_map(
        body,
        mesh=mesh,
        in_specs=(P(None, None, "chan", "band"),),
        out_specs=P("chan", "band"),
        check_vma=False,
    )
```

profile of v0, /device:TPU:0, one launch (start us, length us, event | category | flops | bytes accessed | tf_op | source)
XLA Modules:
  0.0 327.6 jit_solution(6133088543758207707)
XLA Ops:
  6.5 0.0 copy-start
  6.5 0.0 all-gather.2.cloned.1.call-start
  6.5 4.2 %copy.37 = bf16[2,8,64,1024]{3,1,0,2:T(8,128)(2,1)} copy(bf16[2,8,64,1024]{3,2,1,0:T(8,128)(2,1)} %param.1) | data formatting | bytes 4194304 | tf_op args[0]
  10.7 0.0 all-gather.2.cloned.1.call-update
  10.8 0.0 copy-done
  10.8 3.2 copy.31
  14.0 0.4 multiply_reduce_fusion.1
  14.4 0.2 copy.40
  14.6 0.1 bitcast_reduce_fusion.1
  14.7 4.0 %fusion.14 = (bf16[1,8,64,1024]{2,3,1,0:T(8,128)(2,1)S(1)}, bf16[1,8,64,1024]{2,3,1,0:T(8,128)(2,1)}) fusion(bf16[2,8,64,1024]{2,3,1,0:T(8,128)(2,1)} %copy.31), kind=kLoop, calls=%fused_computation.25 | loop fusion | flops 524288 | bytes 4194304 | tf_op jit(solution)/shard_map/slice | solution.py:32
  18.7 180.3 %all-gather.2.cloned.1.call-done = bf16[2,8,1024,1024]{3,1,0,2:T(8,128)(2,1)} async-done(((bf16[2,8,64,1024]{3,1,0,2:T(8,128)(2,1)}), bf16[2,8,1024,1024]{3,1,0,2:T(8,128)(2,1)}) %all-gather.2.cloned.1.call-update) | async-done | bytes 33554448 | tf_op jit(solution)/shard_map/all_gather | solution.py:36
  199.1 18.3 %multiply_reduce_fusion = f32[1024,1024]{1,0:T(8,128)} fusion(bf16[2,8,1024,1024]{3,1,0,2:T(8,128)(2,1)} %all-gather.2.cloned.1.call-done), kind=kLoop, calls=%fused_computation | loop fusion | flops 49283072 | bytes 37748736 | tf_op jit(solution)/shard_map/reduce_sum | solution.py:45
  217.3 5.3 %copy.41 = f32[1024,1024]{0,1:T(8,128)} copy(f32[1024,1024]{1,0:T(8,128)} %multiply_reduce_fusion) | data formatting | bytes 8388608 | tf_op jit(solution)/shard_map/reduce_sum | solution.py:45
  222.7 3.1 bitcast_reduce_fusion
  225.8 45.1 %copy.38 = bf16[2,8,1024,1024]{2,3,1,0:T(8,128)(2,1)} copy(bf16[2,8,1024,1024]{3,1,0,2:T(8,128)(2,1)} %all-gather.2.cloned.1.call-done) | data formatting | bytes 67108864 | tf_op jit(solution)/shard_map/all_gather | solution.py:36
  271.0 25.2 %fusion.5 = f32[64,128,1024]{2,1,0:T(8,128)} fusion(bf16[2,8,1024,64,16]{2,4,3,1,0:T(8,128)(2,1)} %bitcast.24, bf16[1,8,64,64,16]{2,4,0,3,1:T(8,128)(2,1)} %bitcast.27, bf16[1,8,64,64,16]{2,4,0,3,1:T(8,128)(2,1)S(1)} %bitcast.26, bf16[2,8,64,64,16]{2,4,3,1,0:T(8,128)(2,1)} %bitcast.25), kind=kOutput, calls=%fused_computation.8 | convolution fusion | flops 4307550208 | bytes 71303168 | tf_op jit(solution)/shard_map/pkinw,pkjnw->nij/dot_general | solution.py:39
  296.2 11.9 %fusion.4 = f32[64,1024]{1,0:T(8,128)S(1)} fusion(f32[64,128,1024]{2,1,0:T(8,128)} %fusion.5, f32[64,1024]{1,0:T(8,128)S(1)} %add_bitcast_fusion, f32[64,64]{1,0:T(8,128)S(1)} %add_bitcast_fusion.1), kind=kLoop, calls=%fused_computation.7 | loop fusion | flops 25100288 | bytes 34095104 | tf_op jit(solution)/shard_map/reduce_sum | solution.py:49
  308.1 0.1 bitcast_select_fusion
  308.3 0.1 copy.42
  308.3 11.8 %all_to_all.5 = f32[8,64,128]{2,1,0:T(8,128)S(1)} all-to-all(f32[8,64,128]{2,1,0:T(8,128)S(1)} %copy.42), channel_id=1, replica_groups=mesh['band'=8,'chan'=16] {'band'}, dimensions={0} | all-to-all | bytes 524288 | tf_op jit(solution)/shard_map/all_to_all | solution.py:19
  320.1 0.6 broadcast_multiply_fusion
  (6 shorter events, 0.1 us)
Async XLA Ops:
  6.5 4.2 %copy-start = (bf16[2,8,64,1024]{3,2,1,0:T(8,128)(2,1)S(1)}, bf16[2,8,64,1024]{3,2,1,0:T(8,128)(2,1)}, u32[]{:S(2)}) copy-start(bf16[2,8,64,1024]{3,2,1,0:T(8,128)(2,1)} %param.1) | copy-start | bytes 6291460
  6.5 192.5 %all-gather.2.cloned.1.call-start = ((), (), s32[]{:S(2)}) async-start(), calls=%async_computation.1 | async-start | bytes 35651584 | tf_op jit(solution)/shard_map/all_gather | solution.py:36
Sparse Core Ops, SparseCore 0:
  10.9 188.1 all-gather.1
where the time goes:
time: 329 us; the launch traced here: 328 us
  waiting for transfers between devices  180 us (55%)
  local copies, waits for them, and re-layouts  58.2 us (18%)
  other arithmetic  38.6 us (12%)
  matrix products  25.2 us (8%)
  between operations  13.5 us (4%)
  blocking collectives  11.8 us (4%)
    all_gather x1, waiting for transfers between devices, body(): piece = lax.all_gather(coeffs, 'chan', axis=2, tiled=True)  180 us
    all_gather x1, local copies, waits for them, and re-layouts, body(): piece = lax.all_gather(coeffs, 'chan', axis=2, tiled=True)  45.1 us
    dot_general x1, matrix products, body(): jnp.einsum('pkinw,pkjnw->nij', left_side, right_side, preferred_element_t...  25.2 us
    reduce_sum x2, other arithmetic, body(): piece_power = jnp.sum(wide_piece * wide_piece, axis=(0, 1, 4)).T + epsilon  21.4 us
    reduce_sum x1, other arithmetic, body(): partial_value = jnp.sum(coh_band, axis=0)  11.9 us
    all_to_all x1, blocking collectives, sent_and_summed(): lax.all_to_all(in_blocks(shard, dim, length), axis, 0, 0, tiled=True)  11.8 us
    unnamed x5, local copies, waits for them, and re-layouts  7.43 us
  transfers between devices with their start and end apart: 1, of which 1 were waited for; matrix products, arithmetic and copies ran while one was open for 2% of the time, Pallas kernels for 0%

commit v1 on v0

--- a/solution.py
+++ b/solution.py
@@ -33,7 +33,7 @@
     left_side = jnp.concatenate((local_rows, paired), axis=2)
     wide_rows = local_rows.astype(jnp.float32)
     own_power = jnp.sum(wide_rows * wide_rows, axis=(0, 1, 4)).T + epsilon
-    piece = lax.all_gather(coeffs, "chan", axis=2, tiled=True)
+    piece = jnp.concatenate(jax.lax.all_gather(coeffs, "chan"), axis=2)
     count = piece.shape[2]
     right_side = piece.reshape(2, K, count, num_bands, W)
     product = jnp.einsum(

time: 329 us -> 459 us (1.40)
  local copies, waits for them, and re-layouts: 58.2 us -> 177 us
  other arithmetic: 38.6 us -> 45 us
    another operation x0 -> x1, local copies, waits for them, and re-layouts: none -> 86.9 us  [body(): right_side = piece.reshape(2, K, count, num_bands, W)]
    all_gather x1, local copies, waits for them, and re-layouts: 45.1 us -> 77.6 us  [body(): piece = jnp.concatenate(jax.lax.all_gather(coeffs, 'chan'), axis=2)]
    reduce_sum x2, other arithmetic: 21.4 us -> 27.8 us  [body(): piece_power = jnp.sum(wide_piece * wide_piece, axis=(0, 1, 4)).T + epsilon]
where the time goes in v1:
time: 459 us; the launch traced here: 455 us
  waiting for transfers between devices  182 us (40%)
  local copies, waits for them, and re-layouts  177 us (39%)
  other arithmetic  45 us (10%)
  matrix products  25.2 us (5%)
  between operations  13.5 us (3%)
  blocking collectives  11.8 us (3%)
    all_gather x1, waiting for transfers between devices, body(): piece = jnp.concatenate(jax.lax.all_gather(coeffs, 'chan'), axis=2)  181 us
    another operation x1, local copies, waits for them, and re-layouts, body(): right_side = piece.reshape(2, K, count, num_bands, W)  86.9 us
    all_gather x1, local copies, waits for them, and re-layouts, body(): piece = jnp.concatenate(jax.lax.all_gather(coeffs, 'chan'), axis=2)  77.6 us
    reduce_sum x2, other arithmetic, body(): piece_power = jnp.sum(wide_piece * wide_piece, axis=(0, 1, 4)).T + epsilon  27.8 us
    dot_general x1, matrix products, body(): jnp.einsum('pkinw,pkjnw->nij', left_side, right_side, preferred_element_t...  25.2 us
    reduce_sum x1, other arithmetic, body(): partial_value = jnp.sum(coh_band, axis=0)  11.9 us
    all_to_all x1, blocking collectives, sent_and_summed(): lax.all_to_all(in_blocks(shard, dim, length), axis, 0, 0, tiled=True)  11.8 us
  transfers between devices with their start and end apart: 1, of which 1 were waited for; matrix products, arithmetic and copies ran while one was open for 2% of the time, Pallas kernels for 0%

profile of v1, /device:TPU:0, one launch (start us, length us, event | category | flops | bytes accessed | tf_op | source)
XLA Modules:
  0.0 454.5 jit_solution(1168359111608429131)
XLA Ops:
  6.5 0.0 copy-start
  6.5 0.0 all-gather.3.cloned.1.call-start
  6.5 0.7 all-gather.3.cloned.1.call-update
  7.3 4.8 %copy.19 = bf16[2,8,64,1024]{2,3,1,0:T(8,128)(2,1)} copy(bf16[2,8,64,1024]{3,2,1,0:T(8,128)(2,1)} %param.1) | data formatting | bytes 4194304 | tf_op args[0]
  12.0 0.0 copy-done
  12.0 0.4 multiply_reduce_fusion.1
  12.5 0.2 copy.27
  12.7 0.1 bitcast_reduce_fusion
  12.8 3.9 fusion.14
  16.7 181.2 %all-gather.3.cloned.1.call-done = bf16[32,8,64,1024]{3,2,1,0:T(8,128)(2,1)} async-done(((bf16[2,8,64,1024]{3,2,1,0:T(8,128)(2,1)}), bf16[32,8,64,1024]{3,2,1,0:T(8,128)(2,1)}) %all-gather.3.cloned.1.call-update) | async-done | bytes 33554448 | tf_op jit(solution)/shard_map/all_gather | solution.py:36
  198.0 77.6 %copy.25 = bf16[16,2,8,64,1024]{3,0,4,2,1:T(8,128)(2,1)} copy(bf16[16,2,8,64,1024]{4,3,2,1,0:T(8,128)(2,1)} %bitcast.31) | data formatting | bytes 67108864 | tf_op jit(solution)/shard_map/all_gather | solution.py:36
  275.6 24.7 %multiply_reduce_fusion = f32[16,64,1024]{1,0,2:T(8,128)} fusion(bf16[16,2,8,64,1024]{3,0,4,2,1:T(8,128)(2,1)} %copy.25), kind=kLoop, calls=%fused_computation | loop fusion | flops 49283072 | bytes 37748736 | tf_op jit(solution)/shard_map/reduce_sum | solution.py:45
  300.3 7.6 %reduce_sum.56 = f32[1024,64,16]{0,2,1:T(8,128)} reshape(f32[16,64,1024]{1,0,2:T(8,128)} %multiply_reduce_fusion) | data formatting | bytes 8388608 | tf_op jit(solution)/shard_map/reduce_sum | solution.py:45
  307.9 3.1 reduce_sum.57
  311.0 86.9 %reshape_reshape.3 = bf16[2,8,1024,64,16]{2,4,3,1,0:T(8,128)(2,1)} reshape(bf16[2,8,16,64,1024]{3,2,4,1,0:T(8,128)(2,1)} %bitcast.6) | data formatting | bytes 67108864 | tf_op jit(solution)/shard_map/reshape;reshape | solution.py:38
  397.9 25.2 %fusion.5 = f32[64,128,1024]{2,1,0:T(8,128)} fusion(bf16[2,8,1024,64,16]{2,4,3,1,0:T(8,128)(2,1)} %reshape_reshape.3, bf16[1,8,64,64,16]{2,4,0,3,1:T(8,128)(2,1)} %bitcast.33, bf16[1,8,64,64,16]{2,4,0,3,1:T(8,128)(2,1)S(1)} %bitcast.32, bf16[2,8,64,64,16]{2,4,3,1,0:T(8,128)(2,1)} %bitcast.30), kind=kOutput, calls=%fused_computation.8 | convolution fusion | flops 4307550208 | bytes 71303168 | tf_op jit(solution)/shard_map/pkinw,pkjnw->nij/dot_general | solution.py:39
  423.1 11.9 %fusion.4 = f32[64,1024]{1,0:T(8,128)S(1)} fusion(f32[64,128,1024]{2,1,0:T(8,128)} %fusion.5, f32[64,1024]{1,0:T(8,128)S(1)} %add_bitcast_fusion, f32[64,64]{1,0:T(8,128)S(1)} %add_bitcast_fusion.1), kind=kLoop, calls=%fused_computation.7 | loop fusion | flops 25100288 | bytes 34095104 | tf_op jit(solution)/shard_map/reduce_sum | solution.py:49
  435.1 0.1 bitcast_select_fusion
  435.2 0.1 copy.28
  435.3 11.8 %all_to_all.5 = f32[8,64,128]{2,1,0:T(8,128)S(1)} all-to-all(f32[8,64,128]{2,1,0:T(8,128)S(1)} %copy.28), channel_id=1, replica_groups=mesh['band'=8,'chan'=16] {'band'}, dimensions={0} | all-to-all | bytes 524288 | tf_op jit(solution)/shard_map/all_to_all | solution.py:19
  447.1 0.6 broadcast_multiply_fusion
  (6 shorter events, 0.1 us)
Async XLA Ops:
  6.5 5.5 %copy-start = (bf16[2,8,64,1024]{3,2,1,0:T(8,128)(2,1)S(1)}, bf16[2,8,64,1024]{3,2,1,0:T(8,128)(2,1)}, u32[]{:S(2)}) copy-start(bf16[2,8,64,1024]{3,2,1,0:T(8,128)(2,1)} %param.1) | copy-start | bytes 6291460
  6.5 191.4 %all-gather.3.cloned.1.call-start = ((), (), s32[]{:S(2)}) async-start(), calls=%async_computation.1 | async-start | bytes 35651584 | tf_op jit(solution)/shard_map/all_gather | solution.py:36
Sparse Core Ops, SparseCore 0:
  9.8 188.1 all-gather.2
